TPU v7x, 32 devices: a whole 2x2x4 slice. The times are simulated.
32 devices in a mesh: dp: 4 (over y, x), expert: 8 (over z, core).
Axes of the slice: x: 2, y: 2, z: 4, core: 2. Of those that a mesh axis runs over, the one named last changes fastest.
Arguments:
- out_grad: bfloat16 [512, 3072], P('expert', 'dp'), may hold values from -6 to 6
- gate_probs: bfloat16 [512, 2], P('expert'), may hold values from 0.049804688 to 1
- expert_ids: int32 [512, 2], P('expert'), may hold values from 0 to 3, all different within a row; in each aligned block of 64 rows (0 to 63, 64 to 127, ...) at most 40 rows name the same one
- saved_gate: bfloat16 [8, 320, 8192], P('expert', None, 'dp'), may hold values from -8 to 8
- saved_up: bfloat16 [8, 320, 8192], P('expert', None, 'dp'), may hold values from -6 to 6
- w_gate: bfloat16 [8, 3072, 8192], P('expert', None, 'dp'), may hold values from -0.109375 to 0.109375
- w_up: bfloat16 [8, 3072, 8192], P('expert', None, 'dp'), may hold values from -0.109375 to 0.109375
- w_down: bfloat16 [8, 8192, 3072], P('expert', 'dp'), may hold values from -0.046875 to 0.046875
Outputs:
- token_grads: bfloat16 [512, 3072], P('expert', 'dp')
Inputs may be any that keep to these rules, and one draw needn't show every extreme that they name: `expert_ids`: the 2 ids of a row differ. Within the rows of one device (aligned blocks of 64 rows) no expert is named by more than 40 rows, a bound that some block reaches.
All inputs are finite; a program needn't handle non-finite values.
Results may differ from a plain program's by a relative error of at most 0.013.
Values may be sent and summed in bfloat16 or wider, within the bound.
A program may use at most 128 MiB of HBM per device.

v0:
```python
import jax
import jax.numpy as jnp
from jax import lax
from jax.sharding import PartitionSpec as P

SPLIT = 2


def local(out_grad, gate_probs, expert_ids, saved_gate, saved_up, w_gate, w_up, w_down):
    groups = lax.axis_size("expert")
    experts = groups // SPLIT
    columns = out_grad.shape[1]
    tok_rows = out_grad.shape[0]
    slot_count = saved_gate.shape[1]
    capacity = slot_count // groups
    experts_iota = jnp.arange(experts, dtype=jnp.int32)
    chosen = (expert_ids[:, :, None] == experts_iota[None, None, :]).astype(jnp.int32)
    per_token = jnp.sum(chosen, axis=1, dtype=jnp.int32)
    ranked = jnp.cumsum(per_token, axis=0, dtype=jnp.int32) - per_token
    position = jnp.sum(chosen * ranked[:, None, :], axis=2, dtype=jnp.int32)
    target = expert_ids * capacity + position
    slot_iota = jnp.arange(experts * capacity, dtype=jnp.int32)
    matches = slot_iota[:, None, None] == target[None, :, :]
    picker = jnp.any(matches, axis=2).astype(jnp.bfloat16)
    picker = jnp.repeat(picker.reshape(experts, capacity, tok_rows), SPLIT, axis=0).reshape(
        groups * capacity, tok_rows
    )
    weighted = jnp.where(matches, gate_probs.astype(jnp.float32)[None, :, :], 0.0)
    prob_slots = jnp.sum(weighted, axis=(1, 2)).astype(jnp.bfloat16).reshape(experts, capacity)
    prob_slots = jnp.repeat(prob_slots, SPLIT, axis=0)
    down_here = w_down[0]
    dispatched = jnp.dot(picker, out_grad, preferred_element_type=jnp.float32).astype(jnp.bfloat16)
    arrived, arrived_probs = (
        lax.all_to_all(
            dispatched.reshape(groups, capacity, columns),
            "expert",
            split_axis=0,
            concat_axis=0,
            tiled=True,
        ),
        lax.all_to_all(prob_slots, "expert", split_axis=0, concat_axis=0, tiled=True),
    )
    projected = lax.dot_general(
        lax.all_gather(arrived.reshape(slot_count, columns), "dp", axis=1, tiled=True),
        down_here,
        (((1,), (1,)), ((), ())),
        preferred_element_type=jnp.float32,
    )
    gate_pre = saved_gate[0].astype(jnp.float32)
    up_pre = saved_up[0].astype(jnp.float32)
    sigmoid_gate = jax.nn.sigmoid(gate_pre)
    hidden_grad = arrived_probs.reshape(slot_count).astype(jnp.float32)[:, None] * projected
    gate_grad = (
        hidden_grad * up_pre * sigmoid_gate * (1.0 + gate_pre * (1.0 - sigmoid_gate))
    ).astype(jnp.bfloat16)
    up_grad = (hidden_grad * gate_pre * sigmoid_gate).astype(jnp.bfloat16)
    gate_here = w_gate[0]
    up_here = w_up[0]
    first = lax.dot_general(
        gate_here, gate_grad, (((1,), (1,)), ((), ())), preferred_element_type=jnp.float32
    )
    second = lax.dot_general(
        up_here, up_grad, (((1,), (1,)), ((), ())), preferred_element_type=jnp.float32
    )
    shares = lax.psum_scatter(first + second, "dp", scatter_dimension=0, tiled=True)
    returned = lax.all_to_all(
        shares.astype(jnp.bfloat16).reshape(columns, groups, capacity),
        "expert",
        split_axis=1,
        concat_axis=1,
        tiled=True,
    )
    summed = jnp.dot(
        returned.reshape(columns, groups * capacity), picker, preferred_element_type=jnp.float32
    )
    return summed.T.astype(jnp.bfloat16)


def solution(mesh):
    in_specs = (
        P("expert", "dp"),
        P("expert", None),
        P("expert", None),
        P("expert", None, "dp"),
        P("expert", None, "dp"),
        P("expert", None, "dp"),
        P("expert", None, "dp"),
        P("expert", "dp", None),
    )
    out_specs = P("expert", "dp")
    return jax.shard_map(local, mesh=mesh, in_specs=in_specs, out_specs=out_specs, check_vma=False)
```

profile of v0, /device:TPU:0, one launch (start us, length us, event | category | flops | bytes accessed | tf_op | source)
XLA Modules:
  0.0 174.3 jit_solution(16940848212067241526)
XLA Ops:
  6.5 0.7 convert_reduce_fusion.1
  7.3 0.1 copy.24
  7.4 0.1 reduce_window_sum.11
  7.5 0.1 copy.26
  7.5 0.7 select_reduce_fusion.1
  8.3 0.7 multiply_add_fusion
  8.9 0.1 fusion.31
  9.0 0.1 copy.27
  9.2 0.3 convolution_convert_fusion
  9.5 20.9 %all_to_all.19 = bf16[8,40,768]{2,1,0:T(8,128)(2,1)} all-to-all(bf16[8,40,768]{2,1,0:T(8,128)(2,1)S(1)} %bitcast.48), channel_id=1, replica_groups=mesh['dp'=4,'expert'=8] {'expert'}, dimensions={0} | all-to-all | bytes 983040 | tf_op jit(solution)/shard_map/all_to_all | solution.py:34
  30.4 0.0 reduce-scatter.2.cloned.1.call-start
  30.4 0.1 select_reduce_fusion
  30.5 0.1 convert_element_type.62
  30.7 8.0 %all_to_all.20 = bf16[8,1,40]{2,1,0:T(2,128)(2,1)S(1)} all-to-all(bf16[8,1,40]{2,1,0:T(2,128)(2,1)S(1)} %copy.28), channel_id=1, replica_groups=mesh['dp'=4,'expert'=8] {'expert'}, dimensions={0} | all-to-all | bytes 1280 | tf_op jit(solution)/shard_map/all_to_all | solution.py:41
  38.6 0.1 reshape.53
  38.7 24.9 %all-gather.2.cloned.1.call-done = bf16[320,3072]{1,0:T(8,128)(2,1)} async-done(((bf16[320,768]{1,0:T(8,128)(2,1)}), bf16[320,3072]{1,0:T(8,128)(2,1)}) %all-gather.2.cloned.1.call-update) | async-done | bytes 1966096 | tf_op jit(solution)/shard_map/all_gather | solution.py:44
  63.6 7.9 %fusion.12 = f32[320,2048]{1,0:T(8,128)S(1)} fusion(bf16[320,3072]{1,0:T(8,128)(2,1)} %all-gather.2.cloned.1.call-done, bf16[1,2048,3072]{2,1,0:T(8,128)(2,1)} %param.15, f32[320]{0:T(512)S(1)} %reshape.53), kind=kOutput, calls=%fused_computation.11 | convolution fusion | flops 4027187200 | bytes 17171712 | tf_op jit(solution)/shard_map/dot_general | solution.py:43
  71.4 1.5 copy-done.4
  72.9 9.5 %fusion = f32[320,3072]{1,0:T(8,128)} fusion(bf16[1,3072,2048]{2,1,0:T(8,128)(2,1)} %param.14, f32[320,2048]{1,0:T(8,128)S(1)} %fusion.12, bf16[1,320,2048]{2,1,0:T(8,128)(2,1)S(1)} %copy-done.1), kind=kOutput, calls=%fused_computation | convolution fusion | flops 4031119360 | bytes 20447232 | tf_op jit(solution)/shard_map/dot_general | solution.py:62
  82.4 13.3 %fusion.9 = f32[3072,320]{0,1:T(8,128)} fusion(f32[320,3072]{1,0:T(8,128)} %fusion, bf16[1,3072,2048]{2,1,0:T(8,128)(2,1)} %param.13, f32[320,2048]{1,0:T(8,128)} %copy-done.4, bf16[1,320,2048]{2,1,0:T(8,128)(2,1)S(1)} %copy-done.2, bf16[1,320,2048]{2,1,0:T(8,128)(2,1)S(1)} %copy-done.1), kind=kOutput, calls=%fused_computation.7 | convolution fusion | flops 4035379200 | bytes 25690112 | tf_op jit(solution)/shard_map/dot_general | solution.py:59
  95.7 50.6 %reduce-scatter.2.cloned.1.call-done = f32[768,320]{0,1:T(8,128)} async-done(((f32[3072,320]{0,1:T(8,128)}), f32[768,320]{0,1:T(8,128)}) %reduce-scatter.2.cloned.1.call-update) | async-done | bytes 983056 | tf_op jit(solution)/shard_map/reduce_scatter | solution.py:65
  146.3 1.3 convert_element_type.72
  147.6 19.0 %all_to_all.21 = bf16[768,8,40]{0,2,1:T(8,128)(2,1)S(1)} all-to-all(bf16[768,8,40]{0,2,1:T(8,128)(2,1)S(1)} %bitcast.47), channel_id=1, replica_groups=mesh['dp'=4,'expert'=8] {'expert'}, dimensions={1} | all-to-all | bytes 983040 | tf_op jit(solution)/shard_map/all_to_all | solution.py:66
  166.6 0.9 convolution_convert_fusion.1
  (19 shorter events, 0.1 us)
Async XLA Ops:
  6.5 2.6 %copy-start = (bf16[64,768]{1,0:T(8,128)(2,1)S(1)}, bf16[64,768]{1,0:T(8,128)(2,1)}, u32[]{:S(2)}) copy-start(bf16[64,768]{1,0:T(8,128)(2,1)} %param.8) | copy-start | bytes 294916
  6.5 23.9 %copy-start.3 = (bf16[64,2]{0,1:T(2,128)(2,1)S(1)}, bf16[64,2]{0,1:T(2,128)(2,1)}, u32[]{:S(2)}) copy-start(bf16[64,2]{0,1:T(2,128)(2,1)} %param.9) | copy-start | bytes 772
  6.5 57.0 %all-gather.2.cloned.1.call-start = ((), (), s32[]{:S(2)}) async-start(), calls=%async_computation.4 | async-start | bytes 2457600 | tf_op jit(solution)/shard_map/all_gather | solution.py:44
  30.4 115.9 %reduce-scatter.2.cloned.1.call-start = ((), (), s32[]{:S(2)}) async-start(), calls=%async_computation.5 | async-start | bytes 4915200 | tf_op jit(solution)/shard_map/reduce_scatter | solution.py:65
  38.7 34.2 %copy-start.1 = (bf16[1,320,2048]{2,1,0:T(8,128)(2,1)S(1)}, bf16[1,320,2048]{2,1,0:T(8,128)(2,1)}, u32[]{:S(2)}) copy-start(bf16[1,320,2048]{2,1,0:T(8,128)(2,1)} %param.11) | copy-start | bytes 3932164
  71.4 1.5 copy-start.4
  72.9 9.5 %copy-start.2 = (bf16[1,320,2048]{2,1,0:T(8,128)(2,1)S(1)}, bf16[1,320,2048]{2,1,0:T(8,128)(2,1)}, u32[]{:S(2)}) copy-start(bf16[1,320,2048]{2,1,0:T(8,128)(2,1)} %param.12) | copy-start | bytes 3932164
Sparse Core Ops, SparseCore 0:
  30.5 33.0 all-gather.1
  95.8 50.4 reduce-scatter.1
where the time goes:
time: 175 us; the launch traced here: 174 us
  waiting for transfers between devices  75.5 us (43%)
  blocking collectives  47.9 us (27%)
  matrix products  31.8 us (18%)
  between operations  13.5 us (8%)
  other arithmetic  3.69 us (2%)
  local copies, waits for them, and re-layouts  1.99 us (1%)
    reduce_scatter x1, waiting for transfers between devices, local(): lax.psum_scatter(first + second, 'dp', scatter_dimension=0, tiled=True)  50.6 us
    all_gather x1, waiting for transfers between devices, local(): lax.all_gather(arrived.reshape(slot_count, columns), 'dp', axis=1, tiled=...  24.9 us
    all_to_all x1, blocking collectives, local(): lax.all_to_all(dispatched.reshape(groups, capacity, columns), 'expert', s...  20.9 us
    all_to_all x1, blocking collectives, local(): lax.all_to_all(shares.astype(jnp.bfloat16).reshape(columns, groups, capac...  19 us
    dot_general x1, matrix products, local(): lax.dot_general(gate_here, gate_grad, (((1,), (1,)), ((), ())), preferred...  13.3 us
    dot_general x1, matrix products, local(): lax.dot_general(up_here, up_grad, (((1,), (1,)), ((), ())), preferred_ele...  9.48 us
    all_to_all x1, blocking collectives, local(): lax.all_to_all(prob_slots, 'expert', split_axis=0, concat_axis=0, tiled=T...  7.95 us
    dot_general x1, matrix products, local(): lax.dot_general(lax.all_gather(arrived.reshape(slot_count, columns), 'dp'...  7.85 us
  transfers between devices with their start and end apart: 2, of which 2 were waited for; matrix products, arithmetic and copies ran while one was open for 0% of the time, Pallas kernels for 0%

commit v1 on v0

--- a/solution.py
+++ b/solution.py
@@ -1,12 +1,262 @@
+import functools
+
 import jax
 import jax.numpy as jnp
 from jax import lax
+from jax.experimental import pallas as pl
+from jax.experimental.pallas import tpu as pltpu
 from jax.sharding import PartitionSpec as P
 
 SPLIT = 2
+MESH = pl.DeviceIdType.MESH
+TILE = 256
+NT = (((1,), (1,)), ((), ()))
+RETURN_ORDER = (3, 1, 2, 0)
+
+
+def layer_kernel(
+    experts, capacity, columns, hidden,
+    ids_ref, ids_t_ref, probs_t_ref, grad_ref, gate_hbm, up_hbm, wg_hbm, wu_hbm, wd_hbm,
+    out_ref,
+    wd_v, wg_v, wu_v, gate_v, up_v, disp, zrecv, xbuf, xs, acc, gg, ug,
+    pbuf, mine, pair_send, pair_recv, rs_send, rs_recv, back_send, back_recv,
+    wd_sem, wg_sem, wu_sem, saved_sem,
+    z_ss, z_rs, x_ss, x_rs, f_ss, f_rs, pair_ss, pair_rs, rs_ss, rs_rs, b_ss, b_rs,
+):
+    groups = experts * SPLIT
+    tokens = grad_ref.shape[0]
+    d = lax.axis_index("dp")
+    g = lax.axis_index("expert")
+    z, c = g // SPLIT, g % SPLIT
+    sibling = z * SPLIT + (1 - c)
+    dx, dy = d % 2, d // 2
+    peers = (d, dy * 2 + (1 - dx), (1 - dy) * 2 + dx, (1 - dy) * 2 + (1 - dx))
+
+    def block(r):
+        return pl.ds(pl.multiple_of(peers[r] * columns, columns), columns)
+
+    wd_copy = [pltpu.make_async_copy(wd_hbm.at[0, :, block(r)], wd_v.at[r], wd_sem.at[r]) for r in range(4)]
+    wg_copy = [pltpu.make_async_copy(wg_hbm.at[0, block(r), :], wg_v.at[r], wg_sem.at[r]) for r in range(4)]
+    wu_copy = [pltpu.make_async_copy(wu_hbm.at[0, block(r), :], wu_v.at[r], wu_sem.at[r]) for r in range(4)]
+    gate_copy = pltpu.make_async_copy(gate_hbm.at[0], gate_v, saved_sem.at[0])
+    up_copy = pltpu.make_async_copy(up_hbm.at[0], up_v, saved_sem.at[1])
+    barrier = pltpu.get_barrier_semaphore()
+    for k in range(1, experts):
+        pl.semaphore_signal(
+            barrier, inc=1, device_id=(d, ((z + k) % experts) * SPLIT + c), device_id_type=MESH
+        )
+    for r in range(1, 4):
+        pl.semaphore_signal(barrier, inc=1, device_id=(peers[r], g), device_id_type=MESH)
+    pl.semaphore_signal(barrier, inc=1, device_id=(d, sibling), device_id_type=MESH)
+    for copy in wd_copy + [gate_copy, up_copy]:
+        copy.start()
+    for r in RETURN_ORDER:
+        wg_copy[r].start()
+        wu_copy[r].start()
+
+    row = lax.broadcasted_iota(jnp.int32, (tokens, tokens), 0)
+    col = lax.broadcasted_iota(jnp.int32, (tokens, tokens), 1)
+    before = (row < col).astype(jnp.bfloat16)
+    expert_row = lax.broadcasted_iota(jnp.int32, (8, tokens), 0)
+    first, second = ids_t_ref[0:1, :] == expert_row, ids_t_ref[1:2, :] == expert_row
+    named = jnp.where(first | second, 1.0, 0.0)
+    weight = jnp.where(first, probs_t_ref[0:1, :], 0.0) + jnp.where(second, probs_t_ref[1:2, :], 0.0)
+    rank = jnp.dot(named.astype(jnp.bfloat16), before, preferred_element_type=jnp.float32)
+    place = lax.broadcasted_iota(jnp.int32, (capacity, tokens), 0).astype(jnp.float32)
+    for e in range(experts):
+        picked = jnp.where(place == rank[e : e + 1, :], weight[e : e + 1, :], 0.0)
+        disp[e] = jnp.dot(
+            picked.astype(jnp.bfloat16), grad_ref[...], preferred_element_type=jnp.float32
+        ).astype(jnp.bfloat16)
+
+    pl.semaphore_wait(barrier, experts + 3)
+
+    def remote(src, dst, send, recv, device):
+        return pltpu.make_async_remote_copy(
+            src_ref=src, dst_ref=dst, send_sem=send, recv_sem=recv, device_id=device, device_id_type=MESH
+        )
+
+    def z_copies(src, dst, send, recv):
+        copies = []
+        for k in range(1, experts):
+            to = (z + k) % experts
+            copies.append(remote(src.at[to], dst.at[z], send.at[k], recv.at[k], (d, to * SPLIT + c)))
+        return copies
+
+    out_z = z_copies(disp, zrecv, z_ss, z_rs)
+    for copy in out_z:
+        copy.start()
+    zrecv[z] = disp[z]
+    for copy in out_z:
+        copy.wait_recv()
+    xbuf[0, c] = jnp.concatenate(
+        [zrecv[s].astype(jnp.float32) for s in range(experts)], axis=0
+    ).astype(jnp.bfloat16)
+    out_x = [None] + [
+        remote(xbuf.at[0, c], xbuf.at[r, c], x_ss.at[r], x_rs.at[r], (peers[r], g)) for r in range(1, 4)
+    ]
+    forward = [
+        remote(xbuf.at[r, c], xbuf.at[r, c], f_ss.at[r], f_rs.at[r], (d, sibling)) for r in range(4)
+    ]
+    for r in (3, 1, 2):
+        out_x[r].start()
+    forward[0].start()
+
+    def load_slots(r):
+        halves = [xbuf[r, h].astype(jnp.float32) for h in range(SPLIT)]
+        xs[...] = jnp.concatenate(
+            [halves[i % SPLIT][(i // SPLIT) * capacity : (i // SPLIT + 1) * capacity] for i in range(groups)],
+            axis=0,
+        ).astype(jnp.bfloat16)
+
+    for r in range(4):
+        if r + 1 < 4:
+            out_x[r + 1].wait_recv()
+            forward[r + 1].start()
+        forward[r].wait_recv()
+        load_slots(r)
+        wd_copy[r].wait()
+        if r == 3:
+            gate_copy.wait()
+            up_copy.wait()
+
+        def project(n, carry, r=r):
+            here = pl.ds(pl.multiple_of(n * TILE, TILE), TILE)
+            part = lax.dot_general(xs[...], wd_v[r, here, :], NT, preferred_element_type=jnp.float32)
+            if r > 0:
+                part = acc[:, here] + part
+            if r < 3:
+                acc[:, here] = part
+            else:
+                gate = gate_v[:, here].astype(jnp.float32)
+                up = up_v[:, here].astype(jnp.float32)
+                sig = jax.nn.sigmoid(gate)
+                scaled = part * sig
+                gg[:, here] = (scaled * up * (1.0 + gate * (1.0 - sig))).astype(jnp.bfloat16)
+                ug[:, here] = (scaled * gate).astype(jnp.bfloat16)
+            return carry
+
+        lax.fori_loop(0, hidden // TILE, project, 0)
+
+    pair = [
+        remote(pair_send.at[r], pair_recv.at[r], pair_ss.at[r], pair_rs.at[r], (d, sibling)) for r in range(4)
+    ]
+    out_rs = [None] + [
+        remote(rs_send.at[r], rs_recv.at[r], rs_ss.at[r], rs_rs.at[r], (peers[r], g)) for r in range(1, 4)
+    ]
+
+    def pass_on(r):
+        pair[r].wait_recv()
+        rs_send[r] = (mine[r] + pair_recv[r].astype(jnp.float32)).astype(jnp.bfloat16)
+        out_rs[r].start()
+
+    last = None
+    for r in RETURN_ORDER:
+        wg_copy[r].wait()
+        wu_copy[r].wait()
+
+        def back(n, carry, r=r):
+            here = pl.ds(pl.multiple_of(n * TILE, TILE), TILE)
+            part = lax.dot_general(gg[...], wg_v[r, here, :], NT, preferred_element_type=jnp.float32)
+            part = part + lax.dot_general(ug[...], wu_v[r, here, :], NT, preferred_element_type=jnp.float32)
+            for i in range(groups):
+                pbuf[i, :, here] = part[i * capacity : (i + 1) * capacity]
+            return carry
+
+        lax.fori_loop(0, columns // TILE, back, 0)
+        pair_send[r] = jnp.concatenate(
+            [pbuf[s * SPLIT + (1 - c)] for s in range(experts)], axis=0
+        ).astype(jnp.bfloat16)
+        pair[r].start()
+        mine[r] = jnp.concatenate([pbuf[s * SPLIT + c] for s in range(experts)], axis=0)
+        if last is not None:
+            pass_on(last)
+        last = r
+
+    pair[0].wait_recv()
+    total = mine[0] + pair_recv[0].astype(jnp.float32)
+    for r in (1, 2, 3):
+        out_rs[r].wait_recv()
+        total = total + rs_recv[r].astype(jnp.float32)
+    for s in range(experts):
+        back_send[s] = total[s * capacity : (s + 1) * capacity].astype(jnp.bfloat16)
+    out_b = z_copies(back_send, back_recv, b_ss, b_rs)
+    for copy in out_b:
+        copy.start()
+    back_recv[z] = back_send[z]
+
+    after = (col < row).astype(jnp.bfloat16)
+    expert_col = lax.broadcasted_iota(jnp.int32, (tokens, 128), 1)
+    named_t = (ids_ref[:, 0:1] == expert_col) | (ids_ref[:, 1:2] == expert_col)
+    named_t = jnp.where(named_t, 1.0, 0.0)
+    rank_t = jnp.dot(after, named_t.astype(jnp.bfloat16), preferred_element_type=jnp.float32)
+    place_t = lax.broadcasted_iota(jnp.int32, (tokens, capacity), 1).astype(jnp.float32)
+    pickers = [
+        jnp.where(place_t == rank_t[:, e : e + 1], named_t[:, e : e + 1], 0.0).astype(jnp.bfloat16)
+        for e in range(experts)
+    ]
+    for copy in out_b:
+        copy.wait_recv()
+    result = jnp.dot(pickers[0], back_recv[0], preferred_element_type=jnp.float32)
+    for e in range(1, experts):
+        result = result + jnp.dot(pickers[e], back_recv[e], preferred_element_type=jnp.float32)
+    out_ref[...] = result.astype(jnp.bfloat16)
+    for copy in out_z + out_x[1:] + forward + pair + out_rs[1:] + out_b:
+        copy.wait_send()
 
 
 def local(out_grad, gate_probs, expert_ids, saved_gate, saved_up, w_gate, w_up, w_down):
+    groups = lax.axis_size("expert")
+    experts = groups // SPLIT
+    tokens, columns = out_grad.shape
+    slots, hidden = saved_gate.shape[1:]
+    capacity = slots // groups
+    half = experts * capacity
+    vmem = pl.BlockSpec(memory_space=pltpu.VMEM)
+    hbm = pl.BlockSpec(memory_space=pl.ANY)
+    bf16, f32 = jnp.bfloat16, jnp.float32
+    dma = pltpu.SemaphoreType.DMA
+    return pl.pallas_call(
+        functools.partial(layer_kernel, experts, capacity, columns, hidden),
+        out_shape=jax.ShapeDtypeStruct((tokens, columns), bf16),
+        in_specs=[vmem] * 4 + [hbm] * 5,
+        out_specs=vmem,
+        scratch_shapes=[
+            pltpu.VMEM((4, hidden, columns), bf16),
+            pltpu.VMEM((4, columns, hidden), bf16),
+            pltpu.VMEM((4, columns, hidden), bf16),
+            pltpu.VMEM((slots, hidden), bf16),
+            pltpu.VMEM((slots, hidden), bf16),
+            pltpu.VMEM((experts, capacity, columns), bf16),
+            pltpu.VMEM((experts, capacity, columns), bf16),
+            pltpu.VMEM((4, SPLIT, half, columns), bf16),
+            pltpu.VMEM((slots, columns), bf16),
+            pltpu.VMEM((slots, hidden), f32),
+            pltpu.VMEM((slots, hidden), bf16),
+            pltpu.VMEM((slots, hidden), bf16),
+            pltpu.VMEM((groups, capacity, columns), f32),
+            pltpu.VMEM((4, half, columns), f32),
+            pltpu.VMEM((4, half, columns), bf16),
+            pltpu.VMEM((4, half, columns), bf16),
+            pltpu.VMEM((4, half, columns), bf16),
+            pltpu.VMEM((4, half, columns), bf16),
+            pltpu.VMEM((experts, capacity, columns), bf16),
+            pltpu.VMEM((experts, capacity, columns), bf16),
+            dma((4,)), dma((4,)), dma((4,)), dma((2,)),
+            dma((experts,)), dma((experts,)),
+            dma((4,)), dma((4,)), dma((4,)), dma((4,)), dma((4,)), dma((4,)), dma((4,)), dma((4,)),
+            dma((experts,)), dma((experts,)),
+        ],
+        compiler_params=pltpu.CompilerParams(
+            collective_id=0, has_side_effects=True, vmem_limit_bytes=67043328
+        ),
+    )(
+        expert_ids, expert_ids.T, gate_probs.T.astype(f32), out_grad,
+        saved_gate, saved_up, w_gate, w_up, w_down,
+    )
+
+
+def plain_local(out_grad, gate_probs, expert_ids, saved_gate, saved_up, w_gate, w_up, w_down):
     groups = lax.axis_size("expert")
     experts = groups // SPLIT
     columns = out_grad.shape[1]
@@ -76,6 +326,23 @@
     return summed.T.astype(jnp.bfloat16)
 
 
+def kernel_fits(out_grad, saved_gate):
+    columns, hidden = out_grad.shape[1], saved_gate.shape[2]
+    return (
+        lax.axis_size("dp") == 4
+        and lax.axis_size("expert") // SPLIT <= 8
+        and columns % TILE == 0
+        and hidden % TILE == 0
+        and saved_gate.shape[1] % 16 == 0
+        and (saved_gate.shape[1] // lax.axis_size("expert")) % 8 == 0
+        and 4 * 3 * columns * hidden * 2 <= 40 * 2**20
+    )
+
+
+def either(*args):
+    return (local if kernel_fits(args[0], args[3]) else plain_local)(*args)
+
+
 def solution(mesh):
     in_specs = (
         P("expert", "dp"),
@@ -88,4 +355,4 @@
         P("expert", "dp", None),
     )
     out_specs = P("expert", "dp")
-    return jax.shard_map(local, mesh=mesh, in_specs=in_specs, out_specs=out_specs, check_vma=False)
+    return jax.shard_map(either, mesh=mesh, in_specs=in_specs, out_specs=out_specs, check_vma=False)

time: 175 us -> 64.1 us (0.37)
  waiting for transfers between devices: 75.5 us -> 0 us
  Pallas kernels: 0 us -> 59.7 us
  blocking collectives: 47.9 us -> 0 us
  matrix products: 31.8 us -> 0 us
  between operations: 13.5 us -> 0.01 us
  other arithmetic: 3.69 us -> 1.24 us
    pallas_call x0 -> x1, Pallas kernels: none -> 59.7 us  [local(): pl.pallas_call(functools.partial(layer_kernel, experts, capacity, columns...]
    reduce_scatter x1 -> x0, waiting for transfers between devices: 50.6 us -> none  [local(): lax.psum_scatter(first + second, 'dp', scatter_dimension=0, tiled=True)]
    all_to_all x3 -> x0, blocking collectives: 47.9 us -> none  [the longest x1 20.9 us: local(): lax.all_to_all(dispatched.reshape(groups, capacity, columns), 'expert', s...]
    dot_general x5 -> x0, matrix products: 31.8 us -> none  [the longest x1 13.3 us: local(): lax.dot_general(gate_here, gate_grad, (((1,), (1,)), ((), ())), preferred...]
    all_gather x1 -> x0, waiting for transfers between devices: 24.9 us -> none  [local(): lax.all_gather(arrived.reshape(slot_count, columns), 'dp', axis=1, tiled=...]
  transfers between devices with their start and end apart: 2 -> 0, of which waited for: 2 -> 0; matrix products, arithmetic and copies ran while one was open for 0% -> 0% of each run, Pallas kernels for 0% -> 0%
where the time goes in v1:
time: 64.1 us; the launch traced here: 63.9 us
  Pallas kernels  59.7 us (93%)
  local copies, waits for them, and re-layouts  2.92 us (5%)
  other arithmetic  1.24 us (2%)
    pallas_call x1, Pallas kernels, local(): pl.pallas_call(functools.partial(layer_kernel, experts, capacity, columns...  59.7 us
    unnamed x2, local copies, waits for them, and re-layouts  2.92 us

profile of v1, /device:TPU:0, one launch (start us, length us, event | category | flops | bytes accessed | tf_op | source)
XLA Modules:
  0.0 63.9 jit_solution(3617246860890904795)
XLA Ops:
  0.0 1.2 %convert_bitcast_fusion.probs_t_ref = f32[2,64]{1,0:T(2,128)} fusion(bf16[64,2]{0,1:T(2,128)(2,1)} %param.9), kind=kLoop, calls=%fused_computation | loop fusion | flops 128 | bytes 768 | tf_op jit(solution)/shard_map/convert_element_type | solution.py:254
  1.2 1.4 %copy.9.ids_ref = s32[64,2]{1,0:T(8,128)} copy(s32[64,2]{0,1:T(2,128)} %param.10) | data formatting | bytes 1024 | tf_op args[2]
  2.6 59.7 %shard_map.82 = bf16[64,768]{1,0:T(8,128)(2,1)} custom-call(s32[64,2]{1,0:T(8,128)} %copy.9.ids_ref, s32[2,64]{1,0:T(2,128)} %bitcast.3, f32[2,64]{1,0:T(2,128)} %convert_bitcast_fusion.probs_t_ref, bf16[64,768]{1,0:T(8,128)(2,1)} %grad_ref.1, bf16[1,320,2048]{2,1,0:T(8,128)(2,1)} %gate_hbm.1, bf16[1,320,2048]{2,1,0:T(8,128)(2,1)} %up_hbm.1, ...), custom_call_target="tpu_custom_call" | custom-call | tf_op jit(solution)/shard_map/pallas_call | solution.py:219
  62.4 1.5 %copy.11 = bf16[64,768]{1,0:T(8,128)(2,1)} copy(bf16[64,768]{1,0:T(8,128)(2,1)} %shard_map.82) | data formatting | bytes 196608

commit v2 on v1

--- a/solution.py
+++ b/solution.py
@@ -18,8 +18,8 @@
     experts, capacity, columns, hidden,
     ids_ref, ids_t_ref, probs_t_ref, grad_ref, gate_hbm, up_hbm, wg_hbm, wu_hbm, wd_hbm,
     out_ref,
-    wd_v, wg_v, wu_v, gate_v, up_v, disp, zrecv, xbuf, xs, acc, gg, ug,
-    pbuf, mine, pair_send, pair_recv, rs_send, rs_recv, back_send, back_recv,
+    wd_v, wg_v, wu_v, gate_v, up_v, disp, xbuf, xs, acc, gg, ug,
+    pbuf, pair_send, pair_recv, rs_send, rs_recv, back_send, back_recv,
     wd_sem, wg_sem, wu_sem, saved_sem,
     z_ss, z_rs, x_ss, x_rs, f_ss, f_rs, pair_ss, pair_rs, rs_ss, rs_rs, b_ss, b_rs,
 ):
@@ -76,51 +76,71 @@
             src_ref=src, dst_ref=dst, send_sem=send, recv_sem=recv, device_id=device, device_id_type=MESH
         )
 
+    source = [(z + experts - k) % experts for k in range(experts)]
+    target = [(z + k) % experts for k in range(experts)]
+
     def z_copies(src, dst, send, recv):
-        copies = []
-        for k in range(1, experts):
-            to = (z + k) % experts
-            copies.append(remote(src.at[to], dst.at[z], send.at[k], recv.at[k], (d, to * SPLIT + c)))
-        return copies
-
-    out_z = z_copies(disp, zrecv, z_ss, z_rs)
-    for copy in out_z:
+        return [None] + [
+            remote(src.at[target[k]], dst.at[z], send.at[k], recv.at[k], (d, target[k] * SPLIT + c))
+            for k in range(1, experts)
+        ]
+
+    out_z = z_copies(disp, xbuf.at[0, c], z_ss, z_rs)
+    for copy in out_z[1:]:
         copy.start()
-    zrecv[z] = disp[z]
-    for copy in out_z:
-        copy.wait_recv()
-    xbuf[0, c] = jnp.concatenate(
-        [zrecv[s].astype(jnp.float32) for s in range(experts)], axis=0
-    ).astype(jnp.bfloat16)
-    out_x = [None] + [
-        remote(xbuf.at[0, c], xbuf.at[r, c], x_ss.at[r], x_rs.at[r], (peers[r], g)) for r in range(1, 4)
+    xbuf[0, c, z] = disp[z]
+
+    def dp_copy(r_from, r_to, k, to):
+        return remote(
+            xbuf.at[r_from, c, source[k]], xbuf.at[r_to, c, source[k]],
+            x_ss.at[r_to, k], x_rs.at[r_to, k], (peers[to], g),
+        )
+
+    out_x = [
+        None,
+        [dp_copy(0, 1, k, 1) for k in range(experts)],
+        [dp_copy(0, 2, k, 2) for k in range(experts)],
+        [dp_copy(1, 3, k, 2) if k % 2 == 0 else dp_copy(2, 3, k, 1) for k in range(experts)],
     ]
     forward = [
-        remote(xbuf.at[r, c], xbuf.at[r, c], f_ss.at[r], f_rs.at[r], (d, sibling)) for r in range(4)
+        [
+            remote(
+                xbuf.at[r, c, source[k]], xbuf.at[r, c, source[k]],
+                f_ss.at[r, k], f_rs.at[r, k], (d, sibling),
+            )
+            for k in range(experts)
+        ]
+        for r in range(4)
     ]
-    for r in (3, 1, 2):
-        out_x[r].start()
-    forward[0].start()
+
+    def own(k):
+        if k > 0:
+            out_z[k].wait_recv()
+        out_x[1][k].start()
+        out_x[2][k].start()
+        forward[0][k].start()
+
+    def arrive(r, k):
+        out_x[r][k].wait_recv()
+        if r == 1 + k % 2:
+            out_x[3][k].start()
+        forward[r][k].start()
 
     def load_slots(r):
-        halves = [xbuf[r, h].astype(jnp.float32) for h in range(SPLIT)]
         xs[...] = jnp.concatenate(
-            [halves[i % SPLIT][(i // SPLIT) * capacity : (i // SPLIT + 1) * capacity] for i in range(groups)],
-            axis=0,
+            [xbuf[r, i % SPLIT, i // SPLIT].astype(jnp.float32) for i in range(groups)], axis=0
         ).astype(jnp.bfloat16)
 
-    for r in range(4):
-        if r + 1 < 4:
-            out_x[r + 1].wait_recv()
-            forward[r + 1].start()
-        forward[r].wait_recv()
+    def project_block(r):
+        for k in range(experts):
+            forward[r][k].wait_recv()
         load_slots(r)
         wd_copy[r].wait()
         if r == 3:
             gate_copy.wait()
             up_copy.wait()
 
-        def project(n, carry, r=r):
+        def project(n, carry):
             here = pl.ds(pl.multiple_of(n * TILE, TILE), TILE)
             part = lax.dot_general(xs[...], wd_v[r, here, :], NT, preferred_element_type=jnp.float32)
             if r > 0:
@@ -138,52 +158,106 @@
 
         lax.fori_loop(0, hidden // TILE, project, 0)
 
+    own(0)
+    for k in range(1, experts):
+        own(k)
+        arrive(1, k - 1)
+        arrive(2, k - 1)
+    project_block(0)
+    arrive(1, experts - 1)
+    arrive(2, experts - 1)
+    arrive(3, 0)
+    project_block(1)
+    for k in range(1, experts - 1):
+        arrive(3, k)
+    project_block(2)
+    arrive(3, experts - 1)
+    project_block(3)
+
     pair = [
         remote(pair_send.at[r], pair_recv.at[r], pair_ss.at[r], pair_rs.at[r], (d, sibling)) for r in range(4)
     ]
+
+    def sum_copy(r, k, to):
+        return remote(
+            rs_send.at[r, target[k]], rs_recv.at[r, target[k]], rs_ss.at[r, k], rs_rs.at[r, k], (peers[to], g)
+        )
+
     out_rs = [None] + [
-        remote(rs_send.at[r], rs_recv.at[r], rs_ss.at[r], rs_rs.at[r], (peers[r], g)) for r in range(1, 4)
+        [sum_copy(r, k, 1 + k % 2 if r == 3 else r) for k in range(experts)] for r in (1, 2, 3)
     ]
-
-    def pass_on(r):
-        pair[r].wait_recv()
-        rs_send[r] = (mine[r] + pair_recv[r].astype(jnp.float32)).astype(jnp.bfloat16)
-        out_rs[r].start()
-
-    last = None
-    for r in RETURN_ORDER:
+    outward = sorted(range(experts), key=lambda k: -min(k, experts - k))
+
+    def both_halves(r, k):
+        return pbuf[r, target[k] * SPLIT + c] + pair_recv[r, target[k]].astype(jnp.float32)
+
+    def pass_on(r, k):
+        value = both_halves(r, k)
+        if r != 3 and r == 2 - k % 2:
+            out_rs[3][k].wait_recv()
+            value = value + rs_recv[3, target[k]].astype(jnp.float32)
+        rs_send[r, target[k]] = value.astype(jnp.bfloat16)
+        out_rs[r][k].start()
+
+    def back_block(r, between):
         wg_copy[r].wait()
         wu_copy[r].wait()
 
-        def back(n, carry, r=r):
+        def back(n, carry):
             here = pl.ds(pl.multiple_of(n * TILE, TILE), TILE)
             part = lax.dot_general(gg[...], wg_v[r, here, :], NT, preferred_element_type=jnp.float32)
             part = part + lax.dot_general(ug[...], wu_v[r, here, :], NT, preferred_element_type=jnp.float32)
             for i in range(groups):
-                pbuf[i, :, here] = part[i * capacity : (i + 1) * capacity]
+                pbuf[r, i, :, here] = part[i * capacity : (i + 1) * capacity]
             return carry
 
-        lax.fori_loop(0, columns // TILE, back, 0)
-        pair_send[r] = jnp.concatenate(
-            [pbuf[s * SPLIT + (1 - c)] for s in range(experts)], axis=0
-        ).astype(jnp.bfloat16)
+        tiles = columns // TILE
+        lax.fori_loop(0, tiles - 1, back, 0)
+        between()
+        lax.fori_loop(tiles - 1, tiles, back, 0)
+        for s in range(experts):
+            pair_send[r, s] = pbuf[r, s * SPLIT + (1 - c)].astype(jnp.bfloat16)
         pair[r].start()
-        mine[r] = jnp.concatenate([pbuf[s * SPLIT + c] for s in range(experts)], axis=0)
-        if last is not None:
-            pass_on(last)
-        last = r
+
+    def pass_diagonal():
+        pair[3].wait_recv()
+        for k in outward:
+            pass_on(3, k)
+
+    def pass_x():
+        pair[1].wait_recv()
+        for k in outward:
+            if k % 2 == 0:
+                pass_on(1, k)
+
+    def pass_y():
+        pair[2].wait_recv()
+        for k in outward:
+            if k % 2 == 1:
+                pass_on(2, k)
+                pass_on(1, k)
+        for k in outward:
+            if k % 2 == 0:
+                pass_on(2, k)
+
+    back_block(3, lambda: None)
+    back_block(1, pass_diagonal)
+    back_block(2, pass_x)
+    back_block(0, pass_y)
 
     pair[0].wait_recv()
-    total = mine[0] + pair_recv[0].astype(jnp.float32)
-    for r in (1, 2, 3):
-        out_rs[r].wait_recv()
-        total = total + rs_recv[r].astype(jnp.float32)
-    for s in range(experts):
-        back_send[s] = total[s * capacity : (s + 1) * capacity].astype(jnp.bfloat16)
     out_b = z_copies(back_send, back_recv, b_ss, b_rs)
-    for copy in out_b:
-        copy.start()
-    back_recv[z] = back_send[z]
+    for k in outward:
+        out_rs[1][k].wait_recv()
+        out_rs[2][k].wait_recv()
+        total = both_halves(0, k)
+        for r in (1, 2):
+            total = total + rs_recv[r, target[k]].astype(jnp.float32)
+        if k > 0:
+            back_send[target[k]] = total.astype(jnp.bfloat16)
+            out_b[k].start()
+        else:
+            back_recv[z] = total.astype(jnp.bfloat16)
 
     after = (col < row).astype(jnp.bfloat16)
     expert_col = lax.broadcasted_iota(jnp.int32, (tokens, 128), 1)
@@ -195,13 +269,13 @@
         jnp.where(place_t == rank_t[:, e : e + 1], named_t[:, e : e + 1], 0.0).astype(jnp.bfloat16)
         for e in range(experts)
     ]
-    for copy in out_b:
+    for copy in out_b[1:]:
         copy.wait_recv()
     result = jnp.dot(pickers[0], back_recv[0], preferred_element_type=jnp.float32)
     for e in range(1, experts):
         result = result + jnp.dot(pickers[e], back_recv[e], preferred_element_type=jnp.float32)
     out_ref[...] = result.astype(jnp.bfloat16)
-    for copy in out_z + out_x[1:] + forward + pair + out_rs[1:] + out_b:
+    for copy in out_z[1:] + sum(out_x[1:] + forward, []) + pair + sum(out_rs[1:], []) + out_b[1:]:
         copy.wait_send()
 
 
@@ -211,7 +285,6 @@
     tokens, columns = out_grad.shape
     slots, hidden = saved_gate.shape[1:]
     capacity = slots // groups
-    half = experts * capacity
     vmem = pl.BlockSpec(memory_space=pltpu.VMEM)
     hbm = pl.BlockSpec(memory_space=pl.ANY)
     bf16, f32 = jnp.bfloat16, jnp.float32
@@ -228,23 +301,22 @@
             pltpu.VMEM((slots, hidden), bf16),
             pltpu.VMEM((slots, hidden), bf16),
             pltpu.VMEM((experts, capacity, columns), bf16),
-            pltpu.VMEM((experts, capacity, columns), bf16),
-            pltpu.VMEM((4, SPLIT, half, columns), bf16),
+            pltpu.VMEM((4, SPLIT, experts, capacity, columns), bf16),
             pltpu.VMEM((slots, columns), bf16),
             pltpu.VMEM((slots, hidden), f32),
             pltpu.VMEM((slots, hidden), bf16),
             pltpu.VMEM((slots, hidden), bf16),
-            pltpu.VMEM((groups, capacity, columns), f32),
-            pltpu.VMEM((4, half, columns), f32),
-            pltpu.VMEM((4, half, columns), bf16),
-            pltpu.VMEM((4, half, columns), bf16),
-            pltpu.VMEM((4, half, columns), bf16),
-            pltpu.VMEM((4, half, columns), bf16),
+            pltpu.VMEM((4, groups, capacity, columns), f32),
+            pltpu.VMEM((4, experts, capacity, columns), bf16),
+            pltpu.VMEM((4, experts, capacity, columns), bf16),
+            pltpu.VMEM((4, experts, capacity, columns), bf16),
+            pltpu.VMEM((4, experts, capacity, columns), bf16),
             pltpu.VMEM((experts, capacity, columns), bf16),
             pltpu.VMEM((experts, capacity, columns), bf16),
             dma((4,)), dma((4,)), dma((4,)), dma((2,)),
             dma((experts,)), dma((experts,)),
-            dma((4,)), dma((4,)), dma((4,)), dma((4,)), dma((4,)), dma((4,)), dma((4,)), dma((4,)),
+            dma((4, experts)), dma((4, experts)), dma((4, experts)), dma((4, experts)),
+            dma((4,)), dma((4,)), dma((4, experts)), dma((4, experts)),
             dma((experts,)), dma((experts,)),
         ],
         compiler_params=pltpu.CompilerParams(

time: 64.1 us -> 58.4 us (0.911)
  Pallas kernels: 59.7 us -> 54.1 us
    pallas_call x1, Pallas kernels: 59.7 us -> 54.1 us  [local(): pl.pallas_call(functools.partial(layer_kernel, experts, capacity, columns...]
where the time goes in v2:
time: 58.4 us; the launch traced here: 58.2 us
  Pallas kernels  54.1 us (93%)
  local copies, waits for them, and re-layouts  2.92 us (5%)
  other arithmetic  1.24 us (2%)
    pallas_call x1, Pallas kernels, local(): pl.pallas_call(functools.partial(layer_kernel, experts, capacity, columns...  54.1 us
    unnamed x2, local copies, waits for them, and re-layouts  2.92 us
    convert_element_type x1, other arithmetic, local(): gate_probs.T.astype(f32)  1.24 us

profile of v2, /device:TPU:0, one launch (start us, length us, event | category | flops | bytes accessed | tf_op | source)
XLA Modules:
  0.0 58.2 jit_solution(8074746585676998996)
XLA Ops:
  0.0 1.2 %convert_bitcast_fusion.probs_t_ref = f32[2,64]{1,0:T(2,128)} fusion(bf16[64,2]{0,1:T(2,128)(2,1)} %param.9), kind=kLoop, calls=%fused_computation | loop fusion | flops 128 | bytes 768 | tf_op jit(solution)/shard_map/convert_element_type | solution.py:326
  1.2 1.4 %copy.9.ids_ref = s32[64,2]{1,0:T(8,128)} copy(s32[64,2]{0,1:T(2,128)} %param.10) | data formatting | bytes 1024 | tf_op args[2]
  2.6 54.1 %shard_map.82 = bf16[64,768]{1,0:T(8,128)(2,1)} custom-call(s32[64,2]{1,0:T(8,128)} %copy.9.ids_ref, s32[2,64]{1,0:T(2,128)} %bitcast.3, f32[2,64]{1,0:T(2,128)} %convert_bitcast_fusion.probs_t_ref, bf16[64,768]{1,0:T(8,128)(2,1)} %grad_ref.1, bf16[1,320,2048]{2,1,0:T(8,128)(2,1)} %gate_hbm.1, bf16[1,320,2048]{2,1,0:T(8,128)(2,1)} %up_hbm.1, ...), custom_call_target="tpu_custom_call" | custom-call | tf_op jit(solution)/shard_map/pallas_call | solution.py:292
  56.7 1.5 %copy.11 = bf16[64,768]{1,0:T(8,128)(2,1)} copy(bf16[64,768]{1,0:T(8,128)(2,1)} %shard_map.82) | data formatting | bytes 196608

commit v3 on v2

--- a/solution.py
+++ b/solution.py
@@ -11,14 +11,15 @@
 MESH = pl.DeviceIdType.MESH
 TILE = 256
 NT = (((1,), (1,)), ((), ()))
+TN = (((0,), (0,)), ((), ()))
 RETURN_ORDER = (3, 1, 2, 0)
 
 
 def layer_kernel(
     experts, capacity, columns, hidden,
-    ids_ref, ids_t_ref, probs_t_ref, grad_ref, gate_hbm, up_hbm, wg_hbm, wu_hbm, wd_hbm,
+    ids_t_ref, probs_t_ref, grad_ref, gate_hbm, up_hbm, wg_hbm, wu_hbm, wd_hbm,
     out_ref,
-    wd_v, wg_v, wu_v, gate_v, up_v, disp, xbuf, xs, acc, gg, ug,
+    wd_v, wg_v, wu_v, gate_v, up_v, disp, xbuf, xs, acc, gate_factor, up_factor, gg, ug,
     pbuf, pair_send, pair_recv, rs_send, rs_recv, back_send, back_recv,
     wd_sem, wg_sem, wu_sem, saved_sem,
     z_ss, z_rs, x_ss, x_rs, f_ss, f_rs, pair_ss, pair_rs, rs_ss, rs_rs, b_ss, b_rs,
@@ -48,7 +49,7 @@
     for r in range(1, 4):
         pl.semaphore_signal(barrier, inc=1, device_id=(peers[r], g), device_id_type=MESH)
     pl.semaphore_signal(barrier, inc=1, device_id=(d, sibling), device_id_type=MESH)
-    for copy in wd_copy + [gate_copy, up_copy]:
+    for copy in [gate_copy, up_copy] + wd_copy:
         copy.start()
     for r in RETURN_ORDER:
         wg_copy[r].start()
@@ -60,7 +61,8 @@
     expert_row = lax.broadcasted_iota(jnp.int32, (8, tokens), 0)
     first, second = ids_t_ref[0:1, :] == expert_row, ids_t_ref[1:2, :] == expert_row
     named = jnp.where(first | second, 1.0, 0.0)
-    weight = jnp.where(first, probs_t_ref[0:1, :], 0.0) + jnp.where(second, probs_t_ref[1:2, :], 0.0)
+    probs = probs_t_ref[...].astype(jnp.float32)
+    weight = jnp.where(first, probs[0:1, :], 0.0) + jnp.where(second, probs[1:2, :], 0.0)
     rank = jnp.dot(named.astype(jnp.bfloat16), before, preferred_element_type=jnp.float32)
     place = lax.broadcasted_iota(jnp.int32, (capacity, tokens), 0).astype(jnp.float32)
     for e in range(experts):
@@ -126,53 +128,57 @@
             out_x[3][k].start()
         forward[r][k].start()
 
-    def load_slots(r):
-        xs[...] = jnp.concatenate(
-            [xbuf[r, i % SPLIT, i // SPLIT].astype(jnp.float32) for i in range(groups)], axis=0
-        ).astype(jnp.bfloat16)
-
-    def project_block(r):
-        for k in range(experts):
-            forward[r][k].wait_recv()
-        load_slots(r)
-        wd_copy[r].wait()
-        if r == 3:
-            gate_copy.wait()
-            up_copy.wait()
+    def project_blocks(blocks):
+        for r in blocks:
+            for k in range(experts):
+                forward[r][k].wait_recv()
+            xs[r % 2] = jnp.concatenate(
+                [xbuf[r, i % SPLIT, i // SPLIT].astype(jnp.float32) for i in range(groups)], axis=0
+            ).astype(jnp.bfloat16)
+            wd_copy[r].wait()
 
         def project(n, carry):
-            here = pl.ds(pl.multiple_of(n * TILE, TILE), TILE)
-            part = lax.dot_general(xs[...], wd_v[r, here, :], NT, preferred_element_type=jnp.float32)
-            if r > 0:
+            here = pl.ds(pl.multiple_of(n * 2 * TILE, 2 * TILE), 2 * TILE)
+            part = None
+            for r in blocks:
+                term = lax.dot_general(xs[r % 2], wd_v[r, here, :], NT, preferred_element_type=jnp.float32)
+                part = term if part is None else part + term
+            if 0 not in blocks:
                 part = acc[:, here] + part
-            if r < 3:
+            if 3 not in blocks:
                 acc[:, here] = part
             else:
-                gate = gate_v[:, here].astype(jnp.float32)
-                up = up_v[:, here].astype(jnp.float32)
-                sig = jax.nn.sigmoid(gate)
-                scaled = part * sig
-                gg[:, here] = (scaled * up * (1.0 + gate * (1.0 - sig))).astype(jnp.bfloat16)
-                ug[:, here] = (scaled * gate).astype(jnp.bfloat16)
+                gg[:, here] = (part * gate_factor[:, here]).astype(jnp.bfloat16)
+                ug[:, here] = (part * up_factor[:, here]).astype(jnp.bfloat16)
             return carry
 
-        lax.fori_loop(0, hidden // TILE, project, 0)
+        lax.fori_loop(0, hidden // TILE // 2, project, 0)
+
+    def factors(n, carry):
+        here = pl.ds(pl.multiple_of(n * TILE, TILE), TILE)
+        gate = gate_v[:, here].astype(jnp.float32)
+        up = up_v[:, here].astype(jnp.float32)
+        sig = jax.nn.sigmoid(gate)
+        gate_factor[:, here] = up * sig * (1.0 + gate * (1.0 - sig))
+        up_factor[:, here] = gate * sig
+        return carry
 
     own(0)
     for k in range(1, experts):
         own(k)
         arrive(1, k - 1)
         arrive(2, k - 1)
-    project_block(0)
+    gate_copy.wait()
+    up_copy.wait()
+    lax.fori_loop(0, hidden // TILE, factors, 0)
+    project_blocks((0,))
     arrive(1, experts - 1)
     arrive(2, experts - 1)
-    arrive(3, 0)
-    project_block(1)
-    for k in range(1, experts - 1):
+    for k in range(experts - 1):
         arrive(3, k)
-    project_block(2)
+    project_blocks((1, 2))
     arrive(3, experts - 1)
-    project_block(3)
+    project_blocks((3,))
 
     pair = [
         remote(pair_send.at[r], pair_recv.at[r], pair_ss.at[r], pair_rs.at[r], (d, sibling)) for r in range(4)
@@ -259,21 +265,15 @@
         else:
             back_recv[z] = total.astype(jnp.bfloat16)
 
-    after = (col < row).astype(jnp.bfloat16)
-    expert_col = lax.broadcasted_iota(jnp.int32, (tokens, 128), 1)
-    named_t = (ids_ref[:, 0:1] == expert_col) | (ids_ref[:, 1:2] == expert_col)
-    named_t = jnp.where(named_t, 1.0, 0.0)
-    rank_t = jnp.dot(after, named_t.astype(jnp.bfloat16), preferred_element_type=jnp.float32)
-    place_t = lax.broadcasted_iota(jnp.int32, (tokens, capacity), 1).astype(jnp.float32)
     pickers = [
-        jnp.where(place_t == rank_t[:, e : e + 1], named_t[:, e : e + 1], 0.0).astype(jnp.bfloat16)
+        jnp.where((place == rank[e : e + 1, :]) & (named[e : e + 1, :] > 0.0), 1.0, 0.0).astype(jnp.bfloat16)
         for e in range(experts)
     ]
     for copy in out_b[1:]:
         copy.wait_recv()
-    result = jnp.dot(pickers[0], back_recv[0], preferred_element_type=jnp.float32)
+    result = lax.dot_general(pickers[0], back_recv[0], TN, preferred_element_type=jnp.float32)
     for e in range(1, experts):
-        result = result + jnp.dot(pickers[e], back_recv[e], preferred_element_type=jnp.float32)
+        result = result + lax.dot_general(pickers[e], back_recv[e], TN, preferred_element_type=jnp.float32)
     out_ref[...] = result.astype(jnp.bfloat16)
     for copy in out_z[1:] + sum(out_x[1:] + forward, []) + pair + sum(out_rs[1:], []) + out_b[1:]:
         copy.wait_send()
@@ -292,7 +292,7 @@
     return pl.pallas_call(
         functools.partial(layer_kernel, experts, capacity, columns, hidden),
         out_shape=jax.ShapeDtypeStruct((tokens, columns), bf16),
-        in_specs=[vmem] * 4 + [hbm] * 5,
+        in_specs=[vmem] * 3 + [hbm] * 5,
         out_specs=vmem,
         scratch_shapes=[
             pltpu.VMEM((4, hidden, columns), bf16),
@@ -302,7 +302,9 @@
             pltpu.VMEM((slots, hidden), bf16),
             pltpu.VMEM((experts, capacity, columns), bf16),
             pltpu.VMEM((4, SPLIT, experts, capacity, columns), bf16),
-            pltpu.VMEM((slots, columns), bf16),
+            pltpu.VMEM((2, slots, columns), bf16),
+            pltpu.VMEM((slots, hidden), f32),
+            pltpu.VMEM((slots, hidden), f32),
             pltpu.VMEM((slots, hidden), f32),
             pltpu.VMEM((slots, hidden), bf16),
             pltpu.VMEM((slots, hidden), bf16),
@@ -323,7 +325,7 @@
             collective_id=0, has_side_effects=True, vmem_limit_bytes=67043328
         ),
     )(
-        expert_ids, expert_ids.T, gate_probs.T.astype(f32), out_grad,
+        expert_ids.T, gate_probs.T, out_grad,
         saved_gate, saved_up, w_gate, w_up, w_down,
     )
 
@@ -404,7 +406,7 @@
         lax.axis_size("dp") == 4
         and lax.axis_size("expert") // SPLIT <= 8
         and columns % TILE == 0
-        and hidden % TILE == 0
+        and hidden % (2 * TILE) == 0
         and saved_gate.shape[1] % 16 == 0
         and (saved_gate.shape[1] // lax.axis_size("expert")) % 8 == 0
         and 4 * 3 * columns * hidden * 2 <= 40 * 2**20

time: 58.4 us -> 51.6 us (0.88)
  Pallas kernels: 54.1 us -> 49.9 us
  local copies, waits for them, and re-layouts: 2.92 us -> 1.54 us
  other arithmetic: 1.24 us -> 0 us
    pallas_call x1, Pallas kernels: 54.1 us -> 49.9 us  [local(): pl.pallas_call(functools.partial(layer_kernel, experts, capacity, columns...]
    unnamed x2 -> x1, local copies, waits for them, and re-layouts: 2.92 us -> 1.54 us
    convert_element_type x1 -> x0, other arithmetic: 1.24 us -> none  [local(): gate_probs.T.astype(f32)]
where the time goes in v3:
time: 51.6 us; the launch traced here: 51.4 us
  Pallas kernels  49.9 us (97%)
  local copies, waits for them, and re-layouts  1.54 us (3%)
    pallas_call x1, Pallas kernels, local(): pl.pallas_call(functools.partial(layer_kernel, experts, capacity, columns...  49.9 us
    unnamed x1, local copies, waits for them, and re-layouts  1.54 us

profile of v3, /device:TPU:0, one launch (start us, length us, event | category | flops | bytes accessed | tf_op | source)
XLA Modules:
  0.0 51.4 jit_solution(11911163537077058343)
XLA Ops:
  0.0 49.9 %shard_map.82 = bf16[64,768]{1,0:T(8,128)(2,1)} custom-call(s32[2,64]{1,0:T(2,128)} %bitcast.2, bf16[2,64]{1,0:T(2,128)(2,1)} %bitcast.3, bf16[64,768]{1,0:T(8,128)(2,1)} %grad_ref.1, bf16[1,320,2048]{2,1,0:T(8,128)(2,1)} %gate_hbm.1, bf16[1,320,2048]{2,1,0:T(8,128)(2,1)} %up_hbm.1, bf16[1,3072,2048]{2,1,0:T(8,128)(2,1)} %wg_hbm.1, ...), custom_call_target="tpu_custom_call" | custom-call | tf_op jit(solution)/shard_map/pallas_call | solution.py:292
  49.9 1.5 %copy.10 = bf16[64,768]{1,0:T(8,128)(2,1)} copy(bf16[64,768]{1,0:T(8,128)(2,1)} %shard_map.82) | data formatting | bytes 196608
